TPU v7x, 128 devices: a whole 4x4x4 slice. The times are simulated.
128 devices in a mesh: row: 8 (over z_lo, x), col: 16 (over y, z_hi, core).
Axes of the slice: x: 4, y: 4, z: 4 (z_hi: 2, z_lo: 2; z = z_hi * 2 + z_lo), core: 2. Of those that a mesh axis runs over, the one named last changes fastest.
Arguments:
- gate_weight: bfloat16 [4608, 36864], P('row', 'col'), may hold values from -8.838835 to 8.838835
- up_weight: bfloat16 [4608, 36864], P('row', 'col'), may hold values from -8.838835 to 8.838835
- routes: int32 [2, 8], replicated, may hold values from 0 to 7, each once within a row
Outputs:
- gate_serving: bfloat16 [4608, 36864], P('col', 'row')
- up_serving: bfloat16 [4608, 36864], P('col', 'row')
- scales: float32 [2, 36864], P(None, 'row')
Inputs may be any that keep to these rules, and one draw needn't show every extreme that they name: Each row of routes names every serving rank's piece once.
All inputs are finite; a program needn't handle non-finite values. Where the computation divides by a largest or mean magnitude, that divisor is 1e-20 or more.
Results may differ from a plain program's by a relative error of at most 0.001.
Values may be sent and summed in bfloat16 or wider, within the bound.
No kernel may reach another device: no remote copies, remote signals or barrier semaphores. Data moves between devices by JAX's collectives and lax.ppermute only.
A program may use at most 64 MiB of HBM per device.

v0:
```python
import jax
import jax.numpy as jnp
from jax import lax
from jax.sharding import Mesh
from jax.sharding import PartitionSpec as P

COL = ("col_0", "col_1", "col_2")
EPSILON = 1e-06
LIMIT = 4.0


def copy_for_each(value, axis):
    devices = lax.axis_size(axis)
    return lax.all_to_all(
        jnp.broadcast_to(value[None], (devices, *value.shape)), axis, 0, 0, tiled=True
    )


def of_everyone(value, axis):
    everything = copy_for_each(value, axis)
    return jnp.max(everything, axis=0)


def in_one(arrays, axis):
    flat, at, outs = (jnp.concatenate([a.reshape(-1) for a in arrays]), 0, [])
    so_far = of_everyone(flat, axis)
    for a in arrays:
        outs.append(so_far[at : at + a.size].reshape(a.shape))
        at += a.size
    return tuple(outs)


def in_order(pieces, dim):
    pieces = jnp.moveaxis(pieces, 0, dim)
    lengths = pieces.shape
    return pieces.reshape(*lengths[:dim], lengths[dim] * lengths[dim + 1], *lengths[dim + 2 :])


def all_blocks(value, axes, order):
    pieces = value
    for k in order:
        pieces = lax.all_gather(pieces, axes[k])
    done = order[::-1]
    back = [done.index(k) for k in range(len(axes))]
    pieces = pieces.transpose(*back, *range(len(axes), pieces.ndim))
    return pieces.reshape(-1, *value.shape)


def gathered_by_axis(value, axes, order, dim):
    return in_order(all_blocks(value, axes, order), dim)


def column_peaks(weight):
    return jnp.max(jnp.abs(weight), axis=0).astype(jnp.float32)


def quantize(weight, peaks):
    factor = LIMIT / (peaks + EPSILON)
    return (weight.astype(jnp.float32) * factor[None, :]).astype(jnp.bfloat16)


def order_pieces(weight, order, pieces):
    height, width = weight.shape
    shaped = weight.reshape(height, pieces, width // pieces)
    return jnp.take(shaped, order, axis=1).reshape(height, width)


def own_piece(peaks, pick, pieces):
    shaped = ((peaks + EPSILON) / LIMIT).reshape(pieces, -1)
    return lax.dynamic_index_in_dim(shaped, pick, 0, keepdims=False)


def shards(gate_weight, up_weight, routes):
    pieces = lax.axis_size("row")
    row_index = lax.axis_index("row")
    gate_peaks, up_peaks = in_one((column_peaks(gate_weight), column_peaks(up_weight)), "row")
    gate_sent = order_pieces(quantize(gate_weight, gate_peaks), routes[0], pieces)
    up_sent = order_pieces(quantize(up_weight, up_peaks), routes[1], pieces)
    gate_serving, up_serving = (
        lax.all_to_all(
            lax.all_to_all(gate_sent, "row", split_axis=1, concat_axis=0, tiled=True),
            COL,
            split_axis=0,
            concat_axis=1,
            tiled=True,
        ),
        lax.all_to_all(
            lax.all_to_all(up_sent, "row", split_axis=1, concat_axis=0, tiled=True),
            COL,
            split_axis=0,
            concat_axis=1,
            tiled=True,
        ),
    )
    chosen = jnp.take(routes, row_index, axis=1)
    local_scales = jnp.stack(
        [own_piece(gate_peaks, chosen[0], pieces), own_piece(up_peaks, chosen[1], pieces)]
    )
    scales = gathered_by_axis(local_scales, COL, (1, 0, 2), 1)
    return (gate_serving, up_serving, scales)


def solution(mesh):
    finer = Mesh(
        mesh.devices.reshape(mesh.shape["row"], 4, 2, 2), ("row", "col_0", "col_1", "col_2")
    )
    return jax.shard_map(
        shards,
        mesh=finer,
        in_specs=(P("row", COL), P("row", COL), P()),
        out_specs=(P(COL, "row"), P(COL, "row"), P(None, "row")),
        check_vma=False,
    )
```

profile of v0, /device:TPU:1, one launch (start us, length us, event | category | flops | bytes accessed | tf_op | source)
XLA Modules:
  0.0 239.6 jit_solution(6475498258166576045)
XLA Ops:
  0.6 0.0 copy-start
  0.6 0.0 copy-start.2
  0.7 3.3 %abs_reduce_fusion = (bf16[2304]{0:T(1024)(128)(2,1)S(1)}, bf16[2304]{0:T(1024)(128)(2,1)S(1)}) fusion(bf16[576,2304]{1,0:T(8,128)(2,1)} %param.6, bf16[576,2304]{1,0:T(8,128)(2,1)} %param.5), kind=kLoop, calls=%fused_computation.6 | loop fusion | flops 5303808 | bytes 5317632 | tf_op jit(solution)/shard_map/reduce_max | solution.py:54
  3.9 0.7 broadcast_in_dim.25
  4.7 6.2 %all-to-all-start = ((f32[8,1,4608]{2,1,0:T(1,128)}), f32[8,1,4608]{2,1,0:T(1,128)S(1)}, u32[]{:S(2)}, u32[]{:S(2)}) async-start(f32[8,1,4608]{2,1,0:T(1,128)} %broadcast_in_dim.25), calls=%async_computation | async-start | bytes 294912 | tf_op jit(solution)/shard_map/all_to_all | solution.py:14
  10.9 0.0 copy-done.2
  10.9 0.0 copy-done
  10.9 3.0 %copy.45 = bf16[576,2304]{0,1:T(8,128)(2,1)} copy(bf16[576,2304]{1,0:T(8,128)(2,1)S(1)} %copy-done) | data formatting | bytes 5308416 | tf_op args[0]
  13.9 2.5 %all-to-all-done = f32[8,1,4608]{2,1,0:T(1,128)S(1)} async-done(((f32[8,1,4608]{2,1,0:T(1,128)}), f32[8,1,4608]{2,1,0:T(1,128)S(1)}, u32[]{:S(2)}, u32[]{:S(2)}) %all-to-all-start) | async-done | bytes 147488 | tf_op jit(solution)/shard_map/all_to_all | solution.py:14
  16.4 0.1 reduce_max.29
  16.5 0.6 fusion
  17.1 2.4 multiply_convert_fusion.1
  19.5 2.5 %gather_fusion = bf16[8,576,288]{1,2,0:T(8,128)(2,1)} fusion(bf16[576,8,288]{0,2,1:T(8,128)(2,1)S(1)} %bitcast.36, s32[1024]{0:T(1024)S(1)} %pad_clamp_fusion.1), kind=kCustom, calls=%fused_computation.clone | custom fusion | bytes 5308448 | tf_op jit(solution)/shard_map/jit(_take)/gather | solution.py:65
  22.1 3.8 %select_bitcast_fusion.1 = bf16[576,8,288]{0,2,1:T(8,128)(2,1)} fusion(bf16[8,576,288]{1,2,0:T(8,128)(2,1)} %gather_fusion, pred[8]{0:T(512)(128)(4,1)S(1)} %get-tuple-element.23), kind=kLoop, calls=%fused_computation.5 | loop fusion | flops 1327104 | bytes 5308424 | tf_op jit(solution)/shard_map/jit(_take)/select_n | solution.py:65
  25.9 0.0 copy-start.1
  25.9 4.7 %all-to-all-start.1 = ((bf16[576,8,288]{0,2,1:T(8,128)(2,1)}), bf16[576,8,288]{0,2,1:T(8,128)(2,1)}, u32[]{:S(2)}, u32[]{:S(2)}) async-start(bf16[576,8,288]{0,2,1:T(8,128)(2,1)} %select_bitcast_fusion.1), calls=%async_computation.1 | async-start | bytes 5898240 | tf_op jit(solution)/shard_map/all_to_all | solution.py:81
  30.6 0.0 copy-done.1
  30.6 3.0 %copy.50 = bf16[576,2304]{0,1:T(8,128)(2,1)} copy(bf16[576,2304]{1,0:T(8,128)(2,1)S(1)} %copy-done.1) | data formatting | bytes 5308416 | tf_op args[1]
  33.6 2.4 multiply_convert_fusion
  36.0 2.6 %gather_fusion.1 = bf16[8,576,288]{1,2,0:T(8,128)(2,1)} fusion(bf16[576,8,288]{0,2,1:T(8,128)(2,1)S(1)} %bitcast.37, s32[1024]{0:T(1024)S(1)} %pad_clamp_fusion), kind=kCustom, calls=%fused_computation.1.clone | custom fusion | bytes 5308448 | tf_op jit(solution)/shard_map/jit(_take)/gather | solution.py:65
  38.6 3.9 %select_bitcast_fusion = bf16[576,8,288]{0,2,1:T(8,128)(2,1)} fusion(bf16[8,576,288]{1,2,0:T(8,128)(2,1)} %gather_fusion.1, pred[8]{0:T(512)(128)(4,1)S(1)} %get-tuple-element.15), kind=kLoop, calls=%fused_computation.4 | loop fusion | flops 1327104 | bytes 5308424 | tf_op jit(solution)/shard_map/jit(_take)/select_n | solution.py:65
  42.4 24.4 %all-to-all-done.1 = bf16[576,8,288]{0,2,1:T(8,128)(2,1)} async-done(((bf16[576,8,288]{0,2,1:T(8,128)(2,1)}), bf16[576,8,288]{0,2,1:T(8,128)(2,1)}, u32[]{:S(2)}, u32[]{:S(2)}) %all-to-all-start.1) | async-done | bytes 2654240 | tf_op jit(solution)/shard_map/all_to_all | solution.py:81
  66.9 4.5 %all-to-all-start.3 = ((bf16[576,8,288]{0,2,1:T(8,128)(2,1)}), bf16[576,8,288]{0,2,1:T(8,128)(2,1)}, u32[]{:S(2)}, u32[]{:S(2)}) async-start(bf16[576,8,288]{0,2,1:T(8,128)(2,1)} %select_bitcast_fusion), calls=%async_computation.3 | async-start | bytes 5898240 | tf_op jit(solution)/shard_map/all_to_all | solution.py:88
  71.3 4.5 %copy.47 = bf16[8,576,288]{1,0,2:T(8,128)(2,1)} copy(bf16[8,576,288]{1,2,0:T(8,128)(2,1)} %bitcast.3) | data formatting | bytes 5308416 | tf_op jit(solution)/shard_map/all_to_all | solution.py:81
  75.8 5.4 %all_to_all.55 = bf16[16,288,288]{1,0,2:T(8,128)(2,1)S(1)} reshape(bf16[8,576,288]{1,0,2:T(8,128)(2,1)} %copy.47) | data formatting | bytes 5308416 | tf_op jit(solution)/shard_map/all_to_all | solution.py:80
  81.2 2.5 %copy.48 = bf16[16,288,288]{1,2,0:T(8,128)(2,1)} copy(bf16[16,288,288]{1,0,2:T(8,128)(2,1)S(1)} %all_to_all.55) | data formatting | bytes 5308416 | tf_op jit(solution)/shard_map/all_to_all | solution.py:80
  83.7 23.9 %all-to-all-done.3 = bf16[576,8,288]{0,2,1:T(8,128)(2,1)} async-done(((bf16[576,8,288]{0,2,1:T(8,128)(2,1)}), bf16[576,8,288]{0,2,1:T(8,128)(2,1)}, u32[]{:S(2)}, u32[]{:S(2)}) %all-to-all-start.3) | async-done | bytes 2654240 | tf_op jit(solution)/shard_map/all_to_all | solution.py:88
  107.6 8.3 %all-to-all-start.2 = ((bf16[16,288,288]{1,2,0:T(8,128)(2,1)}), bf16[16,288,288]{1,2,0:T(8,128)(2,1)S(1)}, u32[]{:S(2)}, u32[]{:S(2)}) async-start(bf16[16,288,288]{1,2,0:T(8,128)(2,1)} %copy.48), calls=%async_computation.2 | async-start | bytes 7077888 | tf_op jit(solution)/shard_map/all_to_all | solution.py:80
  115.9 4.4 %copy.51 = bf16[8,576,288]{1,0,2:T(8,128)(2,1)} copy(bf16[8,576,288]{1,2,0:T(8,128)(2,1)} %bitcast.9) | data formatting | bytes 5308416 | tf_op jit(solution)/shard_map/all_to_all | solution.py:88
  120.3 6.5 %all_to_all.61 = bf16[16,288,288]{1,0,2:T(8,128)(2,1)} reshape(bf16[8,576,288]{1,0,2:T(8,128)(2,1)} %copy.51) | data formatting | bytes 5308416 | tf_op jit(solution)/shard_map/all_to_all | solution.py:87
  126.9 4.6 %copy.52 = bf16[16,288,288]{1,2,0:T(8,128)(2,1)} copy(bf16[16,288,288]{1,0,2:T(8,128)(2,1)} %all_to_all.61) | data formatting | bytes 5308416 | tf_op jit(solution)/shard_map/all_to_all | solution.py:87
  131.4 28.8 %all-to-all-done.2 = bf16[16,288,288]{1,2,0:T(8,128)(2,1)S(1)} async-done(((bf16[16,288,288]{1,2,0:T(8,128)(2,1)}), bf16[16,288,288]{1,2,0:T(8,128)(2,1)S(1)}, u32[]{:S(2)}, u32[]{:S(2)}) %all-to-all-start.2) | async-done | bytes 2654240 | tf_op jit(solution)/shard_map/all_to_all | solution.py:80
  160.2 11.6 %all-to-all-start.4 = ((bf16[16,288,288]{1,2,0:T(8,128)(2,1)}), bf16[16,288,288]{1,2,0:T(8,128)(2,1)}, u32[]{:S(2)}, u32[]{:S(2)}) async-start(bf16[16,288,288]{1,2,0:T(8,128)(2,1)} %copy.52), calls=%async_computation.4 | async-start | bytes 7077888 | tf_op jit(solution)/shard_map/all_to_all | solution.py:87
  171.8 0.2 select_reduce_fusion
  172.0 0.6 fusion.4
  176.4 1.4 div.21
  177.8 0.7 div.19
  178.5 0.7 constant_dynamic-slice_fusion
  179.2 0.7 constant_dynamic-slice_fusion.1
  179.9 19.4 %all-gather.3 = f32[2,2,288]{2,1,0:T(2,128)S(1)} all-gather(f32[1,2,288]{2,1,0:T(2,128)S(1)} %maximum_bitcast_fusion), channel_id=2, replica_groups=mesh['row'=8,'col_0'=4,'col_1'=2,'col_2'=2] {'col_1'}, dimensions={0}, use_global_device_ids=true | all-gather | bytes 6912 | tf_op jit(solution)/shard_map/all_gather | solution.py:42
  199.3 26.1 %all-gather.1 = f32[8,2,288]{2,1,0:T(2,128)S(1)} all-gather(f32[2,2,288]{2,1,0:T(2,128)S(1)} %all-gather.3), channel_id=3, replica_groups=mesh['row'=8,'col_0'=4,'col_1'=2,'col_2'=2] {'col_0'}, dimensions={0}, use_global_device_ids=true | all-gather | bytes 23040 | tf_op jit(solution)/shard_map/all_gather | solution.py:42
  225.5 4.5 %all-gather.2 = f32[8,2,2,288]{3,2,1,0:T(2,128)S(1)} all-gather(f32[4,2,2,288]{3,2,1,0:T(2,128)S(1)} %bitcast.41), channel_id=4, replica_groups=mesh['row'=8,'col_0'=4,'col_1'=2,'col_2'=2] {'col_2'}, dimensions={0}, use_global_device_ids=true | all-gather | bytes 55296 | tf_op jit(solution)/shard_map/all_gather | solution.py:42
  230.0 0.6 copy.55
  230.6 1.5 reshape.79
  232.2 2.8 %copy.56 = bf16[288,4608]{1,0:T(8,128)(2,1)} copy(bf16[288,4608]{0,1:T(8,128)(2,1)S(1)} %bitcast.38) | data formatting | bytes 5308416 | tf_op jit(solution)/shard_map/all_to_all | solution.py:80
  235.0 0.0 all-to-all-done.4
  235.0 4.6 %copy.57 = bf16[288,4608]{1,0:T(8,128)(2,1)} copy(bf16[288,4608]{0,1:T(8,128)(2,1)} %bitcast.11) | data formatting | bytes 5308416 | tf_op jit(solution)/shard_map/all_to_all | solution.py:87
  (6 shorter events, 0.1 us)
Async XLA Ops:
  0.6 10.3 %copy-start = (bf16[576,2304]{1,0:T(8,128)(2,1)S(1)}, bf16[576,2304]{1,0:T(8,128)(2,1)}, u32[]{:S(2)}) copy-start(bf16[576,2304]{1,0:T(8,128)(2,1)} %param.5) | copy-start | bytes 7962628
  0.6 10.2 %copy-start.2 = (s32[2,8]{1,0:T(2,128)S(1)}, s32[2,8]{1,0:T(2,128)}, u32[]{:S(2)}) copy-start(s32[2,8]{1,0:T(2,128)} %param.7) | copy-start | bytes 196
  4.7 11.7 %all-to-all-start = ((f32[8,1,4608]{2,1,0:T(1,128)}), f32[8,1,4608]{2,1,0:T(1,128)S(1)}, u32[]{:S(2)}, u32[]{:S(2)}) async-start(f32[8,1,4608]{2,1,0:T(1,128)} %broadcast_in_dim.25), calls=%async_computation | async-start | bytes 294912 | tf_op jit(solution)/shard_map/all_to_all | solution.py:14
  25.9 4.7 %copy-start.1 = (bf16[576,2304]{1,0:T(8,128)(2,1)S(1)}, bf16[576,2304]{1,0:T(8,128)(2,1)}, u32[]{:S(2)}) copy-start(bf16[576,2304]{1,0:T(8,128)(2,1)} %param.6) | copy-start | bytes 7962628
  25.9 41.0 %all-to-all-start.1 = ((bf16[576,8,288]{0,2,1:T(8,128)(2,1)}), bf16[576,8,288]{0,2,1:T(8,128)(2,1)}, u32[]{:S(2)}, u32[]{:S(2)}) async-start(bf16[576,8,288]{0,2,1:T(8,128)(2,1)} %select_bitcast_fusion.1), calls=%async_computation.1 | async-start | bytes 5898240 | tf_op jit(solution)/shard_map/all_to_all | solution.py:81
  66.9 40.7 %all-to-all-start.3 = ((bf16[576,8,288]{0,2,1:T(8,128)(2,1)}), bf16[576,8,288]{0,2,1:T(8,128)(2,1)}, u32[]{:S(2)}, u32[]{:S(2)}) async-start(bf16[576,8,288]{0,2,1:T(8,128)(2,1)} %select_bitcast_fusion), calls=%async_computation.3 | async-start | bytes 5898240 | tf_op jit(solution)/shard_map/all_to_all | solution.py:88
  107.6 52.6 %all-to-all-start.2 = ((bf16[16,288,288]{1,2,0:T(8,128)(2,1)}), bf16[16,288,288]{1,2,0:T(8,128)(2,1)S(1)}, u32[]{:S(2)}, u32[]{:S(2)}) async-start(bf16[16,288,288]{1,2,0:T(8,128)(2,1)} %copy.48), calls=%async_computation.2 | async-start | bytes 7077888 | tf_op jit(solution)/shard_map/all_to_all | solution.py:80
  160.2 74.8 %all-to-all-start.4 = ((bf16[16,288,288]{1,2,0:T(8,128)(2,1)}), bf16[16,288,288]{1,2,0:T(8,128)(2,1)}, u32[]{:S(2)}, u32[]{:S(2)}) async-start(bf16[16,288,288]{1,2,0:T(8,128)(2,1)} %copy.52), calls=%async_computation.4 | async-start | bytes 7077888 | tf_op jit(solution)/shard_map/all_to_all | solution.py:87
where the time goes:
time: 241 us; the launch traced here: 240 us
  waiting for transfers between devices  79.7 us (33%)
  local copies, waits for them, and re-layouts  53.4 us (22%)
  blocking collectives  50.1 us (21%)
  starting transfers between devices  35.2 us (15%)
  other arithmetic  16.7 us (7%)
  between operations  4.63 us (2%)
    all_gather x3, blocking collectives, all_blocks(): pieces = lax.all_gather(pieces, axes[k])  50.1 us
    all_to_all x1, waiting for transfers between devices, shards(): lax.all_to_all(lax.all_to_all(gate_sent, 'row', split_axis=1, concat_axis...  28.8 us
    all_to_all x1, waiting for transfers between devices, shards(): lax.all_to_all(gate_sent, 'row', split_axis=1, concat_axis=0, tiled=True)  24.4 us
    all_to_all x1, waiting for transfers between devices, shards(): lax.all_to_all(up_sent, 'row', split_axis=1, concat_axis=0, tiled=True)  23.9 us
    all_to_all x3, local copies, waits for them, and re-layouts, shards(): lax.all_to_all(lax.all_to_all(up_sent, 'row', split_axis=1, concat_axis=0...  15.8 us
    all_to_all x1, starting transfers between devices, shards(): lax.all_to_all(lax.all_to_all(up_sent, 'row', split_axis=1, concat_axis=0...  11.6 us
    all_to_all x3, local copies, waits for them, and re-layouts, shards(): lax.all_to_all(lax.all_to_all(gate_sent, 'row', split_axis=1, concat_axis...  10.7 us
    all_to_all x1, starting transfers between devices, shards(): lax.all_to_all(lax.all_to_all(gate_sent, 'row', split_axis=1, concat_axis...  8.29 us
  transfers between devices with their start and end apart: 5, of which 4 were waited for; matrix products, arithmetic and copies ran while one was open for 17% of the time, Pallas kernels for 0%

commit v1 on v0

--- a/solution.py
+++ b/solution.py
@@ -77,12 +77,20 @@
     gate_sent = order_pieces(quantize(gate_weight, gate_peaks), routes[0], pieces)
     up_sent = order_pieces(quantize(up_weight, up_peaks), routes[1], pieces)
     gate_serving, up_serving = (
-        lax.all_to_all(
-            lax.all_to_all(gate_sent, "row", split_axis=1, concat_axis=0, tiled=True),
-            COL,
-            split_axis=0,
-            concat_axis=1,
-            tiled=True,
+        jnp.concatenate(
+            lax.all_to_all(
+                jnp.stack(
+                    jnp.split(
+                        lax.all_to_all(gate_sent, "row", split_axis=1, concat_axis=0, tiled=True),
+                        lax.axis_size(COL),
+                        axis=0,
+                    )
+                ),
+                COL,
+                0,
+                0,
+            ),
+            axis=1,
         ),
         lax.all_to_all(
             lax.all_to_all(up_sent, "row", split_axis=1, concat_axis=0, tiled=True),

time: 241 us -> 241 us (level)
  waiting for transfers between devices: 79.7 us -> 70.2 us
  local copies, waits for them, and re-layouts: 53.4 us -> 62.7 us
    unnamed x8 -> x23, local copies, waits for them, and re-layouts: 5.95 us -> 17.8 us
    all_to_all x3 -> x0, local copies, waits for them, and re-layouts: 10.7 us -> none  [shards(): lax.all_to_all(lax.all_to_all(gate_sent, 'row', split_axis=1, concat_axis...]
    all_to_all x1, waiting for transfers between devices: 23.9 us -> 14.5 us  [shards(): lax.all_to_all(up_sent, 'row', split_axis=1, concat_axis=0, tiled=True)]
    all_to_all x1 -> x2, local copies, waits for them, and re-layouts: 4.46 us -> 9 us  [shards(): lax.all_to_all(gate_sent, 'row', split_axis=1, concat_axis=0, tiled=True)]
    reshape x0 -> x1, local copies, waits for them, and re-layouts: none -> 2.82 us  [shards(): jnp.concatenate(lax.all_to_all(jnp.stack(jnp.split(lax.all_to_all(gate_se...]
  transfers between devices with their start and end apart: 5 -> 5, of which waited for: 4 -> 4; matrix products, arithmetic and copies ran while one was open for 17% -> 21% of each run, Pallas kernels for 0% -> 0%
where the time goes in v1:
time: 241 us; the launch traced here: 240 us
  waiting for transfers between devices  70.2 us (29%)
  local copies, waits for them, and re-layouts  62.7 us (26%)
  blocking collectives  50.1 us (21%)
  starting transfers between devices  35.2 us (15%)
  other arithmetic  16.7 us (7%)
  between operations  4.64 us (2%)
    all_gather x3, blocking collectives, all_blocks(): pieces = lax.all_gather(pieces, axes[k])  50.1 us
    all_to_all x1, waiting for transfers between devices, shards(): lax.all_to_all(jnp.stack(jnp.split(lax.all_to_all(gate_sent, 'row', split...  28.8 us
    all_to_all x1, waiting for transfers between devices, shards(): lax.all_to_all(gate_sent, 'row', split_axis=1, concat_axis=0, tiled=True)  24.4 us
    unnamed x23, local copies, waits for them, and re-layouts  17.8 us
    all_to_all x3, local copies, waits for them, and re-layouts, shards(): lax.all_to_all(lax.all_to_all(up_sent, 'row', split_axis=1, concat_axis=0...  15.7 us
    all_to_all x1, waiting for transfers between devices, shards(): lax.all_to_all(up_sent, 'row', split_axis=1, concat_axis=0, tiled=True)  14.5 us
    all_to_all x1, starting transfers between devices, shards(): lax.all_to_all(lax.all_to_all(up_sent, 'row', split_axis=1, concat_axis=0...  11.6 us
    all_to_all x2, local copies, waits for them, and re-layouts, shards(): lax.all_to_all(gate_sent, 'row', split_axis=1, concat_axis=0, tiled=True)  9 us
  transfers between devices with their start and end apart: 5, of which 4 were waited for; matrix products, arithmetic and copies ran while one was open for 21% of the time, Pallas kernels for 0%

profile of v1, /device:TPU:1, one launch (start us, length us, event | category | flops | bytes accessed | tf_op | source)
XLA Modules:
  0.0 239.5 jit_solution(4610531223259248276)
XLA Ops:
  0.6 0.0 copy-start
  0.6 0.0 copy-start.2
  0.7 3.3 %abs_reduce_fusion = (bf16[2304]{0:T(1024)(128)(2,1)S(1)}, bf16[2304]{0:T(1024)(128)(2,1)S(1)}) fusion(bf16[576,2304]{1,0:T(8,128)(2,1)} %param.6, bf16[576,2304]{1,0:T(8,128)(2,1)} %param.5), kind=kLoop, calls=%fused_computation.6 | loop fusion | flops 5303808 | bytes 5317632 | tf_op jit(solution)/shard_map/reduce_max | solution.py:54
  3.9 0.7 broadcast_in_dim.25
  4.7 6.2 %all-to-all-start = ((f32[8,1,4608]{2,1,0:T(1,128)}), f32[8,1,4608]{2,1,0:T(1,128)S(1)}, u32[]{:S(2)}, u32[]{:S(2)}) async-start(f32[8,1,4608]{2,1,0:T(1,128)} %broadcast_in_dim.25), calls=%async_computation | async-start | bytes 294912 | tf_op jit(solution)/shard_map/all_to_all | solution.py:14
  10.9 0.0 copy-done.2
  10.9 0.0 copy-done
  10.9 3.0 %copy.66 = bf16[576,2304]{0,1:T(8,128)(2,1)} copy(bf16[576,2304]{1,0:T(8,128)(2,1)S(1)} %copy-done) | data formatting | bytes 5308416 | tf_op args[0]
  13.9 2.5 %all-to-all-done = f32[8,1,4608]{2,1,0:T(1,128)S(1)} async-done(((f32[8,1,4608]{2,1,0:T(1,128)}), f32[8,1,4608]{2,1,0:T(1,128)S(1)}, u32[]{:S(2)}, u32[]{:S(2)}) %all-to-all-start) | async-done | bytes 147488 | tf_op jit(solution)/shard_map/all_to_all | solution.py:14
  16.4 0.1 reduce_max.29
  16.5 0.6 fusion.16
  17.1 2.4 multiply_convert_fusion.1
  19.5 2.5 %gather_fusion = bf16[8,576,288]{1,2,0:T(8,128)(2,1)} fusion(bf16[576,8,288]{0,2,1:T(8,128)(2,1)S(1)} %bitcast.100, s32[1024]{0:T(1024)S(1)} %pad_clamp_fusion.1), kind=kCustom, calls=%fused_computation.clone | custom fusion | bytes 5308448 | tf_op jit(solution)/shard_map/jit(_take)/gather | solution.py:65
  22.0 3.8 %select_bitcast_fusion.1 = bf16[576,8,288]{0,2,1:T(8,128)(2,1)} fusion(bf16[8,576,288]{1,2,0:T(8,128)(2,1)} %gather_fusion, pred[8]{0:T(512)(128)(4,1)S(1)} %get-tuple-element.23), kind=kLoop, calls=%fused_computation.5 | loop fusion | flops 1327104 | bytes 5308424 | tf_op jit(solution)/shard_map/jit(_take)/select_n | solution.py:65
  25.8 0.0 copy-start.1
  25.8 4.7 %all-to-all-start.1 = ((bf16[576,8,288]{0,2,1:T(8,128)(2,1)}), bf16[576,8,288]{0,2,1:T(8,128)(2,1)}, u32[]{:S(2)}, u32[]{:S(2)}) async-start(bf16[576,8,288]{0,2,1:T(8,128)(2,1)} %select_bitcast_fusion.1), calls=%async_computation.1 | async-start | bytes 5898240 | tf_op jit(solution)/shard_map/all_to_all | solution.py:84
  30.6 0.0 copy-done.1
  30.6 3.0 %copy.72 = bf16[576,2304]{0,1:T(8,128)(2,1)} copy(bf16[576,2304]{1,0:T(8,128)(2,1)S(1)} %copy-done.1) | data formatting | bytes 5308416 | tf_op args[1]
  33.6 2.4 multiply_convert_fusion
  36.0 2.6 %gather_fusion.1 = bf16[8,576,288]{1,2,0:T(8,128)(2,1)} fusion(bf16[576,8,288]{0,2,1:T(8,128)(2,1)S(1)} %bitcast.101, s32[1024]{0:T(1024)S(1)} %pad_clamp_fusion), kind=kCustom, calls=%fused_computation.1.clone | custom fusion | bytes 5308448 | tf_op jit(solution)/shard_map/jit(_take)/gather | solution.py:65
  38.5 3.9 %select_bitcast_fusion = bf16[576,8,288]{0,2,1:T(8,128)(2,1)} fusion(bf16[8,576,288]{1,2,0:T(8,128)(2,1)} %gather_fusion.1, pred[8]{0:T(512)(128)(4,1)S(1)} %get-tuple-element.15), kind=kLoop, calls=%fused_computation.4 | loop fusion | flops 1327104 | bytes 5308424 | tf_op jit(solution)/shard_map/jit(_take)/select_n | solution.py:65
  42.4 24.4 %all-to-all-done.1 = bf16[576,8,288]{0,2,1:T(8,128)(2,1)} async-done(((bf16[576,8,288]{0,2,1:T(8,128)(2,1)}), bf16[576,8,288]{0,2,1:T(8,128)(2,1)}, u32[]{:S(2)}, u32[]{:S(2)}) %all-to-all-start.1) | async-done | bytes 2654240 | tf_op jit(solution)/shard_map/all_to_all | solution.py:84
  66.8 4.4 %all-to-all-start.3 = ((bf16[576,8,288]{0,2,1:T(8,128)(2,1)}), bf16[576,8,288]{0,2,1:T(8,128)(2,1)}, u32[]{:S(2)}, u32[]{:S(2)}) async-start(bf16[576,8,288]{0,2,1:T(8,128)(2,1)} %select_bitcast_fusion), calls=%async_computation.3 | async-start | bytes 5898240 | tf_op jit(solution)/shard_map/all_to_all | solution.py:96
  71.3 4.5 %copy.68 = bf16[8,576,288]{1,0,2:T(8,128)(2,1)} copy(bf16[8,576,288]{1,2,0:T(8,128)(2,1)} %bitcast.3) | data formatting | bytes 5308416 | tf_op jit(solution)/shard_map/all_to_all | solution.py:84
  75.7 4.5 %all_to_all.46 = bf16[4608,288]{0,1:T(8,128)(2,1)S(1)} reshape(bf16[8,576,288]{1,0,2:T(8,128)(2,1)} %copy.68) | data formatting | bytes 5308416 | tf_op jit(solution)/shard_map/all_to_all | solution.py:84
  80.3 0.7 fusion.15
  81.0 0.8 fusion.14
  81.8 0.8 fusion.13
  82.6 0.8 fusion.12
  83.4 0.7 fusion.11
  84.1 0.9 fusion.10
  85.0 0.8 fusion.9
  85.8 0.8 fusion.8
  86.6 0.7 fusion.7
  87.4 0.8 fusion.6
  88.2 0.8 fusion.5
  89.0 0.8 fusion.4
  89.8 0.7 fusion.3
  90.5 0.8 fusion.2
  91.3 0.8 fusion.1
  92.1 0.8 fusion
  93.0 14.5 %all-to-all-done.3 = bf16[576,8,288]{0,2,1:T(8,128)(2,1)} async-done(((bf16[576,8,288]{0,2,1:T(8,128)(2,1)}), bf16[576,8,288]{0,2,1:T(8,128)(2,1)}, u32[]{:S(2)}, u32[]{:S(2)}) %all-to-all-start.3) | async-done | bytes 2654240 | tf_op jit(solution)/shard_map/all_to_all | solution.py:96
  107.5 8.3 %all-to-all-start.2 = ((bf16[16,288,288]{1,2,0:T(8,128)(2,1)}), bf16[16,288,288]{1,2,0:T(8,128)(2,1)S(1)}, u32[]{:S(2)}, u32[]{:S(2)}) async-start(bf16[16,288,288]{1,2,0:T(8,128)(2,1)} %fusion), calls=%async_computation.2 | async-start | bytes 7077888 | tf_op jit(solution)/shard_map/all_to_all | solution.py:81
  115.8 4.5 %copy.73 = bf16[8,576,288]{1,0,2:T(8,128)(2,1)} copy(bf16[8,576,288]{1,2,0:T(8,128)(2,1)} %bitcast.25) | data formatting | bytes 5308416 | tf_op jit(solution)/shard_map/all_to_all | solution.py:96
  120.3 6.5 %all_to_all.50 = bf16[16,288,288]{1,0,2:T(8,128)(2,1)} reshape(bf16[8,576,288]{1,0,2:T(8,128)(2,1)} %copy.73) | data formatting | bytes 5308416 | tf_op jit(solution)/shard_map/all_to_all | solution.py:95
  126.8 4.5 %copy.74 = bf16[16,288,288]{1,2,0:T(8,128)(2,1)} copy(bf16[16,288,288]{1,0,2:T(8,128)(2,1)} %all_to_all.50) | data formatting | bytes 5308416 | tf_op jit(solution)/shard_map/all_to_all | solution.py:95
  131.3 28.8 %all-to-all-done.2 = bf16[16,288,288]{1,2,0:T(8,128)(2,1)S(1)} async-done(((bf16[16,288,288]{1,2,0:T(8,128)(2,1)}), bf16[16,288,288]{1,2,0:T(8,128)(2,1)S(1)}, u32[]{:S(2)}, u32[]{:S(2)}) %all-to-all-start.2) | async-done | bytes 2654240 | tf_op jit(solution)/shard_map/all_to_all | solution.py:81
  160.1 11.6 %all-to-all-start.4 = ((bf16[16,288,288]{1,2,0:T(8,128)(2,1)}), bf16[16,288,288]{1,2,0:T(8,128)(2,1)}, u32[]{:S(2)}, u32[]{:S(2)}) async-start(bf16[16,288,288]{1,2,0:T(8,128)(2,1)} %copy.74), calls=%async_computation.4 | async-start | bytes 7077888 | tf_op jit(solution)/shard_map/all_to_all | solution.py:95
  171.7 0.2 select_reduce_fusion
  171.9 0.6 fusion.20
  176.4 1.4 div.21
  177.7 0.7 div.19
  178.4 0.7 constant_dynamic-slice_fusion
  179.1 0.7 constant_dynamic-slice_fusion.1
  179.8 19.4 %all-gather.3 = f32[2,2,288]{2,1,0:T(2,128)S(1)} all-gather(f32[1,2,288]{2,1,0:T(2,128)S(1)} %maximum_bitcast_fusion), channel_id=2, replica_groups=mesh['row'=8,'col_0'=4,'col_1'=2,'col_2'=2] {'col_1'}, dimensions={0}, use_global_device_ids=true | all-gather | bytes 6912 | tf_op jit(solution)/shard_map/all_gather | solution.py:42
  199.2 26.1 %all-gather.1 = f32[8,2,288]{2,1,0:T(2,128)S(1)} all-gather(f32[2,2,288]{2,1,0:T(2,128)S(1)} %all-gather.3), channel_id=3, replica_groups=mesh['row'=8,'col_0'=4,'col_1'=2,'col_2'=2] {'col_0'}, dimensions={0}, use_global_device_ids=true | all-gather | bytes 23040 | tf_op jit(solution)/shard_map/all_gather | solution.py:42
  225.4 4.5 %all-gather.2 = f32[8,2,2,288]{3,2,1,0:T(2,128)S(1)} all-gather(f32[4,2,2,288]{3,2,1,0:T(2,128)S(1)} %bitcast.105), channel_id=4, replica_groups=mesh['row'=8,'col_0'=4,'col_1'=2,'col_2'=2] {'col_2'}, dimensions={0}, use_global_device_ids=true | all-gather | bytes 55296 | tf_op jit(solution)/shard_map/all_gather | solution.py:42
  229.9 0.6 copy.77
  230.5 1.5 reshape.83
  232.1 2.8 %copy.79 = bf16[288,4608]{1,0:T(8,128)(2,1)} copy(bf16[288,4608]{0,1:T(8,128)(2,1)S(1)} %bitcast.102) | data formatting | bytes 5308416 | tf_op jit(solution)/shard_map/reshape | solution.py:80
  234.9 0.0 all-to-all-done.4
  234.9 4.6 %copy.80 = bf16[288,4608]{1,0:T(8,128)(2,1)} copy(bf16[288,4608]{0,1:T(8,128)(2,1)} %bitcast.27) | data formatting | bytes 5308416 | tf_op jit(solution)/shard_map/all_to_all | solution.py:95
  (6 shorter events, 0.1 us)
Async XLA Ops:
  0.6 10.3 %copy-start = (bf16[576,2304]{1,0:T(8,128)(2,1)S(1)}, bf16[576,2304]{1,0:T(8,128)(2,1)}, u32[]{:S(2)}) copy-start(bf16[576,2304]{1,0:T(8,128)(2,1)} %param.5) | copy-start | bytes 7962628
  0.6 10.2 %copy-start.2 = (s32[2,8]{1,0:T(2,128)S(1)}, s32[2,8]{1,0:T(2,128)}, u32[]{:S(2)}) copy-start(s32[2,8]{1,0:T(2,128)} %param.7) | copy-start | bytes 196
  4.7 11.7 %all-to-all-start = ((f32[8,1,4608]{2,1,0:T(1,128)}), f32[8,1,4608]{2,1,0:T(1,128)S(1)}, u32[]{:S(2)}, u32[]{:S(2)}) async-start(f32[8,1,4608]{2,1,0:T(1,128)} %broadcast_in_dim.25), calls=%async_computation | async-start | bytes 294912 | tf_op jit(solution)/shard_map/all_to_all | solution.py:14
  25.8 4.7 %copy-start.1 = (bf16[576,2304]{1,0:T(8,128)(2,1)S(1)}, bf16[576,2304]{1,0:T(8,128)(2,1)}, u32[]{:S(2)}) copy-start(bf16[576,2304]{1,0:T(8,128)(2,1)} %param.6) | copy-start | bytes 7962628
  25.8 41.0 %all-to-all-start.1 = ((bf16[576,8,288]{0,2,1:T(8,128)(2,1)}), bf16[576,8,288]{0,2,1:T(8,128)(2,1)}, u32[]{:S(2)}, u32[]{:S(2)}) async-start(bf16[576,8,288]{0,2,1:T(8,128)(2,1)} %select_bitcast_fusion.1), calls=%async_computation.1 | async-start | bytes 5898240 | tf_op jit(solution)/shard_map/all_to_all | solution.py:84
  66.8 40.7 %all-to-all-start.3 = ((bf16[576,8,288]{0,2,1:T(8,128)(2,1)}), bf16[576,8,288]{0,2,1:T(8,128)(2,1)}, u32[]{:S(2)}, u32[]{:S(2)}) async-start(bf16[576,8,288]{0,2,1:T(8,128)(2,1)} %select_bitcast_fusion), calls=%async_computation.3 | async-start | bytes 5898240 | tf_op jit(solution)/shard_map/all_to_all | solution.py:96
  107.5 52.6 %all-to-all-start.2 = ((bf16[16,288,288]{1,2,0:T(8,128)(2,1)}), bf16[16,288,288]{1,2,0:T(8,128)(2,1)S(1)}, u32[]{:S(2)}, u32[]{:S(2)}) async-start(bf16[16,288,288]{1,2,0:T(8,128)(2,1)} %fusion), calls=%async_computation.2 | async-start | bytes 7077888 | tf_op jit(solution)/shard_map/all_to_all | solution.py:81
  160.1 74.8 %all-to-all-start.4 = ((bf16[16,288,288]{1,2,0:T(8,128)(2,1)}), bf16[16,288,288]{1,2,0:T(8,128)(2,1)}, u32[]{:S(2)}, u32[]{:S(2)}) async-start(bf16[16,288,288]{1,2,0:T(8,128)(2,1)} %copy.74), calls=%async_computation.4 | async-start | bytes 7077888 | tf_op jit(solution)/shard_map/all_to_all | solution.py:95
